TPU v7x, 32 devices: a whole 2x2x4 slice. The times are simulated.
32 devices in a mesh: group: 1, pool: 1, slab: 32 (over z, y, x, core).
Axes of the slice: x: 2, y: 2, z: 4, core: 2. Of those that a mesh axis runs over, the one named last changes fastest.
Arguments:
- drho_part: float32 [1, 16, 2, 128, 128, 128], P('pool', 'group', None, 'slab'), may hold values from -6 to 6
- fxc: float32 [128, 128, 128], P('slab'), may hold values from -2 to -0.2
- cutoff_mask: int32 [128, 128, 128], P(None, 'slab'), may hold values 0 or 1
- owner_table: int32 [16], P('group'), may hold values from 0 to 15, each once
Outputs:
- dv: float32 [16, 2, 128, 128, 128], P('group', None, 'slab')
Inputs may be any that keep to these rules, and one draw needn't show every extreme that they name: `owner_table`: each perturbation appears in exactly one slot.
All inputs are finite; a program needn't handle non-finite values. No bound on the sum of `cutoff_mask` on one device may be relied on, other than what follows from the above.
Results may differ from a plain program's by a relative error of at most 0.00008.
Values sent between devices are 32-bit elements; how exact they have to be, the bound alone decides.
A program may use at most 128 MiB of HBM per device.

v0:
```python
import functools
import math

import jax
import jax.numpy as jnp
import numpy as np
from jax import lax
from jax.experimental import pallas as pl
from jax.experimental.pallas import tpu as pltpu
from jax.sharding import PartitionSpec as P

CHUNKS = 2
VMEM_MIB = 60
PER_STEP = 2


def halves(matrix):
    high = matrix.astype(np.float32).astype(jnp.bfloat16)
    low = (matrix - high.astype(np.float64)).astype(np.float32).astype(jnp.bfloat16)
    return np.stack([high, low])


def complex_dft(length, sign):
    index = np.arange(length)
    angle = (index[:, None] * index[None, :] % length) * (2.0 * math.pi / length)
    cosine, sine = np.cos(angle), sign * np.sin(angle)
    return np.block([[cosine, -sine], [sine, cosine]])


def slab_order(length, width):
    table = np.arange(2 * length).reshape(2, length // width, width)
    return table.transpose(1, 0, 2).reshape(-1)


def inner_order(length, width):
    table = np.arange(2 * length).reshape(2, length // width, width)
    return table.transpose(2, 0, 1).reshape(-1)


def split(value):
    high = value.astype(jnp.bfloat16)
    low = (value - high.astype(jnp.float32)).astype(jnp.bfloat16)
    return high, low


def dot(left, right):
    return jnp.dot(left, right, preferred_element_type=jnp.float32)


def left_dot(matrix_ref, value):
    high, low = split(value)
    return dot(matrix_ref[0], high) + (dot(matrix_ref[1], high) + dot(matrix_ref[0], low))


def right_dot(value, matrix_ref):
    high, low = split(value)
    return dot(high, matrix_ref[0]) + (dot(low, matrix_ref[0]) + dot(high, matrix_ref[1]))


def forward_kernel(owner_ref, *refs):
    *field_refs, along_z_ref, along_y_ref, out_ref = refs
    _, _, width, length, _ = field_refs[0].shape
    slabs = length // width
    rows = width * length
    fields = [
        jnp.concatenate([ref[0, 0].reshape(rows, length), ref[0, 1].reshape(rows, length)], axis=1)
        for ref in field_refs
    ]
    fields = [right_dot(field, along_z_ref) for field in fields]
    fields = [
        jnp.concatenate(
            [
                jnp.concatenate(
                    [field[x * length : (x + 1) * length, c * length : (c + 1) * length] for c in range(2)], axis=0
                )
                for x in range(width)
            ],
            axis=1,
        )
        for field in fields
    ]
    fields = [left_dot(along_y_ref, field) for field in fields]
    for slot, field in enumerate(fields):
        for y in range(width):
            for c in range(2):
                first = (y * 2 + c) * slabs
                for x in range(width):
                    out_ref[:, slot, c * width + x, y * length : (y + 1) * length] = field[
                        first : first + slabs, x * length : (x + 1) * length
                    ]


def column_stage(field_ref, screen_ref, forth_ref, back_ref, out_ref):
    slabs, slots, rows, lanes = field_ref.shape
    length = screen_ref.shape[0]
    fields = [field_ref[:, slot].reshape(slabs * rows, lanes) for slot in range(slots)]
    fields = [left_dot(forth_ref, field) for field in fields]
    screen = screen_ref[...]
    fields = [jnp.concatenate([field[:length] * screen, field[length:] * screen], axis=0) for field in fields]
    fields = [left_dot(back_ref, field) for field in fields]
    for slot, field in enumerate(fields):
        out_ref[:, slot] = field.reshape(slabs, rows, lanes)


def backward_kernel(slots, owner_ref, field_ref, *refs):
    density_refs, out_ref = refs[:slots], refs[-1]
    fxc_ref, along_y_ref, along_z_ref = refs[slots : slots + 3]
    _, _, width, length, _ = density_refs[0].shape
    fields = [
        jnp.concatenate(
            [
                jnp.concatenate(
                    [
                        field_ref[:, slot, c * width + x, y * length : (y + 1) * length]
                        for y in range(width)
                        for c in range(2)
                    ],
                    axis=0,
                )
                for x in range(width)
            ],
            axis=1,
        )
        for slot in range(slots)
    ]
    fields = [left_dot(along_y_ref, field) for field in fields]
    fields = [
        jnp.concatenate(
            [
                jnp.concatenate(
                    [field[c * length : (c + 1) * length, x * length : (x + 1) * length] for c in range(2)], axis=1
                )
                for x in range(width)
            ],
            axis=0,
        )
        for field in fields
    ]
    fields = [right_dot(field, along_z_ref) for field in fields]
    fxc = fxc_ref[...]
    for slot, field in enumerate(fields):
        for c in range(2):
            part = field[:, c * length : (c + 1) * length].reshape(width, length, length)
            out_ref[slot, c] = part + fxc * density_refs[slot][0, c]


def frequency(index, length):
    return ((index + length // 2) % length - length // 2).astype(jnp.float32)


def column_screen(cutoff_mask, length):
    width = cutoff_mask.shape[1]
    start = lax.axis_index("slab") * width
    full_index = jnp.arange(length, dtype=jnp.int32)
    part_index = start + jnp.arange(width, dtype=jnp.int32)
    full_square = frequency(full_index, length) ** 2
    part_square = frequency(part_index, length) ** 2
    total = full_square[:, None, None] + part_square[None, :, None] + full_square[None, None, :]
    unit = (2.0 * math.pi / length) ** 2
    screen = 4.0 * math.pi * cutoff_mask.astype(jnp.float32) / (unit * total + 0.25)
    return (screen * (1.0 / float(length**3))).reshape(length, width * length)


def whole_spec(array):
    zeros = (0,) * array.ndim
    return pl.BlockSpec(array.shape, lambda *_: zeros)


def cost(count, rows, length):
    size = 2 * rows * length
    return pl.CostEstimate(flops=count * 24 * size * length, bytes_accessed=count * 8 * size, transcendentals=0)


def per_device(drho_part, fxc, cutoff_mask, owner_table):
    density = drho_part[0]
    if lax.axis_size("pool") > 1:
        density = lax.psum(density, "pool")
    count, _, width, length, _ = density.shape
    slabs = length // width
    rows, lanes = 2 * width, width * length
    chunks = math.gcd(CHUNKS, count)
    each = count // chunks
    slots = math.gcd(PER_STEP, each)
    steps = each // slots

    forth, back = complex_dft(length, -1.0), complex_dft(length, 1.0)
    by_slab, by_inner = slab_order(length, width), inner_order(length, width)
    z_forth, z_back = jnp.asarray(halves(forth.T)), jnp.asarray(halves(back.T))
    y_forth, y_back = jnp.asarray(halves(forth[by_inner])), jnp.asarray(halves(back[:, by_inner]))
    x_forth, x_back = jnp.asarray(halves(forth[:, by_slab])), jnp.asarray(halves(back[by_slab]))
    screen = column_screen(cutoff_mask, length)

    params = pltpu.CompilerParams(dimension_semantics=("arbitrary",), vmem_limit_bytes=VMEM_MIB * 2**20)
    packed = jax.ShapeDtypeStruct((slabs, each, rows, lanes), jnp.float32)
    packed_spec = pl.BlockSpec((slabs, slots, rows, lanes), lambda i, *_: (0, i, 0, 0))
    price = cost(each, lanes, length)

    def owned(chunk, slot):
        return pl.BlockSpec(
            (1, 2, width, length, length), lambda i, owner: (owner[chunk * each + i * slots + slot], 0, 0, 0, 0)
        )

    def forward(chunk):
        return pl.pallas_call(
            forward_kernel,
            out_shape=packed,
            grid_spec=pltpu.PrefetchScalarGridSpec(
                num_scalar_prefetch=1,
                grid=(steps,),
                in_specs=[owned(chunk, slot) for slot in range(slots)]
                + [
                    whole_spec(z_forth),
                    whole_spec(y_forth),
                ],
                out_specs=packed_spec,
            ),
            compiler_params=params,
            cost_estimate=price,
        )(owner_table, *[density] * slots, z_forth, y_forth)

    def columns(field):
        return pl.pallas_call(
            column_stage,
            out_shape=packed,
            grid=(steps,),
            in_specs=[packed_spec, whole_spec(screen), whole_spec(x_forth), whole_spec(x_back)],
            out_specs=packed_spec,
            compiler_params=params,
            cost_estimate=price,
        )(field, screen, x_forth, x_back)

    def backward(chunk, field, result):
        earlier = [] if result is None else [result]
        return pl.pallas_call(
            functools.partial(backward_kernel, slots),
            out_shape=jax.ShapeDtypeStruct(density.shape, jnp.float32),
            grid_spec=pltpu.PrefetchScalarGridSpec(
                num_scalar_prefetch=1,
                grid=(steps,),
                in_specs=[packed_spec]
                + [owned(chunk, slot) for slot in range(slots)]
                + [
                    whole_spec(fxc),
                    whole_spec(y_back),
                    whole_spec(z_back),
                ]
                + [pl.BlockSpec(memory_space=pl.ANY)] * len(earlier),
                out_specs=pl.BlockSpec(
                    (slots, 2, width, length, length), lambda i, owner: (chunk * steps + i, 0, 0, 0, 0)
                ),
            ),
            input_output_aliases={5 + slots: 0} if earlier else {},
            compiler_params=params,
            cost_estimate=price,
        )(owner_table, field, *[density] * slots, fxc, y_back, z_back, *earlier)

    def swap(field):
        return lax.all_to_all(field, "slab", split_axis=0, concat_axis=0, tiled=True)

    spectra = [swap(forward(chunk)) for chunk in range(chunks)]
    spectra = [swap(columns(field)) for field in spectra]
    result = None
    for chunk, field in enumerate(spectra):
        result = backward(chunk, field, result)
    return result


def solution(mesh):
    placed = (
        P("pool", "group", None, "slab", None, None),
        P("slab", None, None),
        P(None, "slab", None),
        P("group"),
    )
    return jax.shard_map(
        per_device,
        mesh=mesh,
        in_specs=placed,
        out_specs=P("group", None, "slab", None, None),
        check_vma=False,
    )
```

profile of v0, /device:TPU:24, one launch (start us, length us, event | category | flops | bytes accessed | tf_op | source)
XLA Modules:
  0.0 410.9 jit_solution(17383635639696737975)
XLA Ops:
  0.0 9.1 %shard_map.102 = f32[32,8,8,512]{3,2,1,0:T(8,128)} custom-call(s32[16]{0:T(128)} %owner_ref.7, f32[16,2,4,128,128]{4,3,2,1,0:T(8,128)} %bitcast.5, f32[16,2,4,128,128]{4,3,2,1,0:T(8,128)} %bitcast.6, bf16[2,256,256]{2,1,0:T(8,128)(2,1)} %constant.57.clone.refs_2_, bf16[2,256,256]{2,1,0:T(8,128)(2,1)} %constant.59.clone.refs_3_), custom_call_target="tpu_custom_call" | custom-call | flops 3221225472 | bytes 8388608 | tf_op jit(solution)/shard_map/pallas_call | solution.py:204
  9.1 5.9 %all-to-all-start.2 = ((f32[32,8,8,512]{3,2,1,0:T(8,128)}), f32[32,8,8,512]{3,2,1,0:T(8,128)}, u32[]{:S(2)}, u32[]{:S(2)}) async-start(f32[32,8,8,512]{3,2,1,0:T(8,128)} %shard_map.102), calls=%async_computation.2 | async-start | bytes 8388608 | tf_op jit(solution)/shard_map/all_to_all | solution.py:258
  15.0 9.0 %shard_map.100 = f32[32,8,8,512]{3,2,1,0:T(8,128)} custom-call(s32[16]{0:T(128)} %owner_ref.7, f32[16,2,4,128,128]{4,3,2,1,0:T(8,128)} %bitcast.7, f32[16,2,4,128,128]{4,3,2,1,0:T(8,128)} %bitcast.8, bf16[2,256,256]{2,1,0:T(8,128)(2,1)} %constant.57.clone.refs_2_, bf16[2,256,256]{2,1,0:T(8,128)(2,1)} %constant.59.clone.refs_3_), custom_call_target="tpu_custom_call" | custom-call | flops 3221225472 | bytes 8388608 | tf_op jit(solution)/shard_map/pallas_call | solution.py:204
  24.0 0.0 copy-start
  24.0 83.5 %all-to-all-done.2.field_ref = f32[32,8,8,512]{3,2,1,0:T(8,128)} async-done(((f32[32,8,8,512]{3,2,1,0:T(8,128)}), f32[32,8,8,512]{3,2,1,0:T(8,128)}, u32[]{:S(2)}, u32[]{:S(2)}) %all-to-all-start.2) | async-done | bytes 4194336 | tf_op jit(solution)/shard_map/all_to_all | solution.py:258
  107.5 5.5 %all-to-all-start = ((f32[32,8,8,512]{3,2,1,0:T(8,128)}), f32[32,8,8,512]{3,2,1,0:T(8,128)}, u32[]{:S(2)}, u32[]{:S(2)}) async-start(f32[32,8,8,512]{3,2,1,0:T(8,128)} %shard_map.100), calls=%async_computation | async-start | bytes 8388608 | tf_op jit(solution)/shard_map/all_to_all | solution.py:258
  113.0 0.1 broadcast_add_fusion
  113.1 0.0 copy-done
  113.1 0.2 fusion
  113.3 0.7 copy.14
  114.0 7.3 %shard_map.103 = f32[32,8,8,512]{3,2,1,0:T(8,128)} custom-call(f32[32,8,8,512]{3,2,1,0:T(8,128)} %all-to-all-done.2.field_ref, f32[128,512]{1,0:T(8,128)} %bitcast.14, bf16[2,256,256]{2,1,0:T(8,128)(2,1)} %constant.61.clone.forth_ref, bf16[2,256,256]{2,1,0:T(8,128)(2,1)} %constant.62.clone.back_ref), custom_call_target="tpu_custom_call" | custom-call | flops 3221225472 | bytes 8388608 | tf_op jit(solution)/shard_map/pallas_call | solution.py:222
  121.3 84.2 %all-to-all-done.field_ref = f32[32,8,8,512]{3,2,1,0:T(8,128)} async-done(((f32[32,8,8,512]{3,2,1,0:T(8,128)}), f32[32,8,8,512]{3,2,1,0:T(8,128)}, u32[]{:S(2)}, u32[]{:S(2)}) %all-to-all-start) | async-done | bytes 4194336 | tf_op jit(solution)/shard_map/all_to_all | solution.py:258
  205.4 5.5 %all-to-all-start.3 = ((f32[32,8,8,512]{3,2,1,0:T(8,128)}), f32[32,8,8,512]{3,2,1,0:T(8,128)}, u32[]{:S(2)}, u32[]{:S(2)}) async-start(f32[32,8,8,512]{3,2,1,0:T(8,128)} %shard_map.103), calls=%async_computation.3 | async-start | bytes 8388608 | tf_op jit(solution)/shard_map/all_to_all | solution.py:258
  210.9 7.3 %shard_map.101 = f32[32,8,8,512]{3,2,1,0:T(8,128)} custom-call(f32[32,8,8,512]{3,2,1,0:T(8,128)} %all-to-all-done.field_ref, f32[128,512]{1,0:T(8,128)} %bitcast.15, bf16[2,256,256]{2,1,0:T(8,128)(2,1)} %constant.61.clone.forth_ref, bf16[2,256,256]{2,1,0:T(8,128)(2,1)} %constant.62.clone.back_ref), custom_call_target="tpu_custom_call" | custom-call | flops 3221225472 | bytes 8388608 | tf_op jit(solution)/shard_map/pallas_call | solution.py:222
  218.1 85.2 %all-to-all-done.3.field_ref = f32[32,8,8,512]{3,2,1,0:T(8,128)} async-done(((f32[32,8,8,512]{3,2,1,0:T(8,128)}), f32[32,8,8,512]{3,2,1,0:T(8,128)}, u32[]{:S(2)}, u32[]{:S(2)}) %all-to-all-start.3) | async-done | bytes 4194336 | tf_op jit(solution)/shard_map/all_to_all | solution.py:258
  303.4 5.5 %all-to-all-start.1 = ((f32[32,8,8,512]{3,2,1,0:T(8,128)}), f32[32,8,8,512]{3,2,1,0:T(8,128)}, u32[]{:S(2)}, u32[]{:S(2)}) async-start(f32[32,8,8,512]{3,2,1,0:T(8,128)} %shard_map.101), calls=%async_computation.1 | async-start | bytes 8388608 | tf_op jit(solution)/shard_map/all_to_all | solution.py:258
  308.8 9.6 %shard_map.104.refs_5_ = f32[16,2,4,128,128]{4,3,2,1,0:T(8,128)} custom-call(s32[16]{0:T(128)} %owner_ref.7, f32[32,8,8,512]{3,2,1,0:T(8,128)} %all-to-all-done.3.field_ref, f32[16,2,4,128,128]{4,3,2,1,0:T(8,128)} %bitcast.9, f32[16,2,4,128,128]{4,3,2,1,0:T(8,128)} %bitcast.10, f32[4,128,128]{2,1,0:T(8,128)} %refs_2_.5, ...), custom_call_target="tpu_custom_call" | custom-call | flops 3221225472 | bytes 8388608 | tf_op jit(solution)/shard_map/pallas_call | solution.py:234
  318.4 82.9 %all-to-all-done.1.field_ref = f32[32,8,8,512]{3,2,1,0:T(8,128)} async-done(((f32[32,8,8,512]{3,2,1,0:T(8,128)}), f32[32,8,8,512]{3,2,1,0:T(8,128)}, u32[]{:S(2)}, u32[]{:S(2)}) %all-to-all-start.1) | async-done | bytes 4194336 | tf_op jit(solution)/shard_map/all_to_all | solution.py:258
  401.3 9.6 %shard_map.105 = f32[16,2,4,128,128]{4,3,2,1,0:T(8,128)} custom-call(s32[16]{0:T(128)} %owner_ref.7, f32[32,8,8,512]{3,2,1,0:T(8,128)} %all-to-all-done.1.field_ref, f32[16,2,4,128,128]{4,3,2,1,0:T(8,128)} %bitcast.11, f32[16,2,4,128,128]{4,3,2,1,0:T(8,128)} %bitcast.12, f32[4,128,128]{2,1,0:T(8,128)} %refs_2_.5, ...), custom_call_target="tpu_custom_call", output_to_operand_aliasing={{}: (7, {})} | custom-call | flops 3221225472 | bytes 8388608 | tf_op jit(solution)/shard_map/pallas_call | solution.py:234
  (2 shorter events, 0.0 us)
Async XLA Ops:
  9.1 98.4 %all-to-all-start.2 = ((f32[32,8,8,512]{3,2,1,0:T(8,128)}), f32[32,8,8,512]{3,2,1,0:T(8,128)}, u32[]{:S(2)}, u32[]{:S(2)}) async-start(f32[32,8,8,512]{3,2,1,0:T(8,128)} %shard_map.102), calls=%async_computation.2 | async-start | bytes 8388608 | tf_op jit(solution)/shard_map/all_to_all | solution.py:258
  24.0 89.1 %copy-start = (s32[128,4,128]{2,1,0:T(4,128)S(1)}, s32[128,4,128]{2,1,0:T(4,128)}, u32[]{:S(2)}) copy-start(s32[128,4,128]{2,1,0:T(4,128)} %param.12) | copy-start | bytes 786436
  107.5 97.9 %all-to-all-start = ((f32[32,8,8,512]{3,2,1,0:T(8,128)}), f32[32,8,8,512]{3,2,1,0:T(8,128)}, u32[]{:S(2)}, u32[]{:S(2)}) async-start(f32[32,8,8,512]{3,2,1,0:T(8,128)} %shard_map.100), calls=%async_computation | async-start | bytes 8388608 | tf_op jit(solution)/shard_map/all_to_all | solution.py:258
  205.4 97.9 %all-to-all-start.3 = ((f32[32,8,8,512]{3,2,1,0:T(8,128)}), f32[32,8,8,512]{3,2,1,0:T(8,128)}, u32[]{:S(2)}, u32[]{:S(2)}) async-start(f32[32,8,8,512]{3,2,1,0:T(8,128)} %shard_map.103), calls=%async_computation.3 | async-start | bytes 8388608 | tf_op jit(solution)/shard_map/all_to_all | solution.py:258
  303.4 97.9 %all-to-all-start.1 = ((f32[32,8,8,512]{3,2,1,0:T(8,128)}), f32[32,8,8,512]{3,2,1,0:T(8,128)}, u32[]{:S(2)}, u32[]{:S(2)}) async-start(f32[32,8,8,512]{3,2,1,0:T(8,128)} %shard_map.101), calls=%async_computation.1 | async-start | bytes 8388608 | tf_op jit(solution)/shard_map/all_to_all | solution.py:258
where the time goes:
time: 415 us; the launch traced here: 411 us
  waiting for transfers between devices  336 us (81%)
  Pallas kernels  51.7 us (12%)
  starting transfers between devices  22.3 us (5%)
    all_to_all x4, waiting for transfers between devices, swap(): lax.all_to_all(field, 'slab', split_axis=0, concat_axis=0, tiled=True)  336 us
    all_to_all x4, starting transfers between devices, swap(): lax.all_to_all(field, 'slab', split_axis=0, concat_axis=0, tiled=True)  22.3 us
    pallas_call x2, Pallas kernels, backward(): pl.pallas_call(functools.partial(backward_kernel, slots), out_shape=jax.S...  19.1 us
    pallas_call x2, Pallas kernels, forward(): pl.pallas_call(forward_kernel, out_shape=packed, grid_spec=pltpu.Prefetch...  18.1 us
    pallas_call x2, Pallas kernels, columns(): pl.pallas_call(column_stage, out_shape=packed, grid=(steps,), in_specs=[p...  14.5 us
  transfers between devices with their start and end apart: 4, of which 4 were waited for; matrix products, arithmetic and copies ran while one was open for 0% of the time, Pallas kernels for 8%

commit v1 on v0

v1 whole, which is shorter than its diff:
```python
import functools
import math

import jax
import jax.numpy as jnp
import numpy as np
from jax import lax
from jax.experimental import pallas as pl
from jax.experimental.pallas import tpu as pltpu
from jax.sharding import PartitionSpec as P

VMEM_MIB = 50
MESH = pl.DeviceIdType.MESH


def halves(matrix):
    high = matrix.astype(np.float32).astype(jnp.bfloat16)
    low = (matrix - high.astype(np.float64)).astype(np.float32).astype(jnp.bfloat16)
    return np.stack([high, low])


def complex_dft(length, sign):
    index = np.arange(length)
    angle = (index[:, None] * index[None, :] % length) * (2.0 * math.pi / length)
    cosine, sine = np.cos(angle), sign * np.sin(angle)
    return np.block([[cosine, -sine], [sine, cosine]])


def slab_order(length, width):
    table = np.arange(2 * length).reshape(2, length // width, width)
    return table.transpose(1, 0, 2).reshape(-1)


def inner_order(length, width):
    table = np.arange(2 * length).reshape(2, length // width, width)
    return table.transpose(2, 0, 1).reshape(-1)


def split(value):
    high = value.astype(jnp.bfloat16)
    low = (value - high.astype(jnp.float32)).astype(jnp.bfloat16)
    return high, low


def dot(left, right):
    return jnp.dot(left, right, preferred_element_type=jnp.float32)


def left_dot(matrix_ref, value):
    high, low = split(value)
    return dot(matrix_ref[0], high) + (dot(matrix_ref[1], high) + dot(matrix_ref[0], low))


def right_dot(value, matrix_ref):
    high, low = split(value)
    return dot(high, matrix_ref[0]) + (dot(low, matrix_ref[0]) + dot(high, matrix_ref[1]))


def forward_stage(field_ref, along_z_ref, along_y_ref, out_ref):
    _, width, length, _ = field_ref.shape
    slabs = length // width
    rows = width * length
    field = jnp.concatenate([field_ref[c].reshape(rows, length) for c in range(2)], axis=1)
    field = right_dot(field, along_z_ref)
    field = jnp.concatenate(
        [
            jnp.concatenate(
                [field[x * length : (x + 1) * length, c * length : (c + 1) * length] for c in range(2)], axis=0
            )
            for x in range(width)
        ],
        axis=1,
    )
    field = left_dot(along_y_ref, field)
    for y in range(width):
        for c in range(2):
            first = (y * 2 + c) * slabs
            for x in range(width):
                out_ref[:, c * width + x, y * length : (y + 1) * length] = field[
                    first : first + slabs, x * length : (x + 1) * length
                ]


def column_stage(field_ref, screen_ref, forth_ref, back_ref, out_ref):
    slabs, rows, lanes = field_ref.shape
    length = screen_ref.shape[0]
    field = left_dot(forth_ref, field_ref[...].reshape(slabs * rows, lanes))
    screen = screen_ref[...]
    field = jnp.concatenate([field[:length] * screen, field[length:] * screen], axis=0)
    out_ref[...] = left_dot(back_ref, field).reshape(slabs, rows, lanes)


def backward_stage(field_ref, fxc_ref, along_y_ref, along_z_ref, out_ref):
    _, width, length, _ = out_ref.shape
    field = jnp.concatenate(
        [
            jnp.concatenate(
                [field_ref[:, c * width + x, y * length : (y + 1) * length] for y in range(width) for c in range(2)],
                axis=0,
            )
            for x in range(width)
        ],
        axis=1,
    )
    field = left_dot(along_y_ref, field)
    field = jnp.concatenate(
        [
            jnp.concatenate(
                [field[c * length : (c + 1) * length, x * length : (x + 1) * length] for c in range(2)], axis=1
            )
            for x in range(width)
        ],
        axis=0,
    )
    field = right_dot(field, along_z_ref)
    fxc = fxc_ref[...]
    for c in range(2):
        part = field[:, c * length : (c + 1) * length].reshape(width, length, length)
        out_ref[c] = part + fxc * out_ref[c]


def frequency(index, length):
    return (lax.rem(index + length // 2, length) - length // 2).astype(jnp.float32)


def fill_screen(mask_ref, screen_ref, me):
    length, width, _ = mask_ref.shape
    shape = (length, length)
    unit = (2.0 * math.pi / length) ** 2
    along_x = frequency(lax.broadcasted_iota(jnp.int32, shape, 0), length)
    along_z = frequency(lax.broadcasted_iota(jnp.int32, shape, 1), length)
    plane = along_x * along_x + along_z * along_z
    for y in range(width):
        along_y = frequency(jnp.full(shape, me * width + y, jnp.int32), length)
        total = unit * (plane + along_y * along_y) + 0.25
        kept = mask_ref[:, y, :].astype(jnp.float32)
        screen_ref[:, y * length : (y + 1) * length] = 4.0 * math.pi * kept / total * (1.0 / float(length**3))


def exchange_kernel(
    density_ref,
    fxc_hbm,
    mask_hbm,
    z_forth_hbm,
    y_forth_hbm,
    x_forth_hbm,
    x_back_hbm,
    y_back_hbm,
    z_back_hbm,
    result_ref,
    out_forth,
    in_forth,
    out_back,
    in_back,
    screen_ref,
    fxc_ref,
    mask_ref,
    z_forth_ref,
    y_forth_ref,
    x_forth_ref,
    x_back_ref,
    y_back_ref,
    z_back_ref,
    load_sem,
    table_sem,
    out_forth_sem,
    in_forth_sem,
    out_back_sem,
    in_back_sem,
):
    count, slabs, _, _ = out_forth.shape
    me = lax.axis_index("slab")

    def load(p):
        return pltpu.make_async_copy(density_ref.at[p], result_ref.at[p], load_sem.at[p])

    pairs = (
        (z_forth_hbm, z_forth_ref),
        (y_forth_hbm, y_forth_ref),
        (mask_hbm, mask_ref),
        (x_forth_hbm, x_forth_ref),
        (x_back_hbm, x_back_ref),
        (fxc_hbm, fxc_ref),
        (y_back_hbm, y_back_ref),
        (z_back_hbm, z_back_ref),
    )
    tables = [pltpu.make_async_copy(source, target, table_sem.at[k]) for k, (source, target) in enumerate(pairs)]

    def send(source, target, out_sem, in_sem, p):
        def one(step, carry):
            peer = lax.rem(me + step, slabs)
            pltpu.make_async_remote_copy(
                source.at[p, peer],
                target.at[p, me],
                out_sem.at[p],
                in_sem.at[p],
                device_id={"slab": peer},
                device_id_type=MESH,
            ).start()
            return carry

        lax.fori_loop(1, slabs, one, 0)

    def whole(source, target, out_sem, in_sem, p):
        others = pl.ds(0, slabs - 1)
        return pltpu.make_async_remote_copy(
            source.at[p, others],
            target.at[p, others],
            out_sem.at[p],
            in_sem.at[p],
            device_id={"slab": me},
            device_id_type=MESH,
        )

    forth = (out_forth, in_forth, out_forth_sem, in_forth_sem)
    back = (out_back, in_back, out_back_sem, in_back_sem)

    load(0).start()
    for table in tables[:2]:
        table.start()
    barrier = pltpu.get_barrier_semaphore()

    def greet(step, carry):
        pl.semaphore_signal(
            barrier, inc=1, device_id={"slab": lax.rem(me + step, slabs)}, device_id_type=MESH
        )
        return carry

    lax.fori_loop(1, slabs, greet, 0)

    def load_rest(p, carry):
        load(p).start()
        return carry

    lax.fori_loop(1, count, load_rest, 0)
    for table in tables[2:]:
        table.start()

    def forward(p):
        load(p).wait()
        forward_stage(result_ref.at[p], z_forth_ref, y_forth_ref, out_forth.at[p])
        in_forth[p, me] = out_forth[p, me]

    for table in tables[:2]:
        table.wait()
    forward(0)
    pl.semaphore_wait(barrier, slabs - 1)
    send(*forth, 0)

    def forward_step(p, carry):
        forward(p)
        send(*forth, p)
        return carry

    lax.fori_loop(1, count, forward_step, 0)

    for table in tables[2:]:
        table.wait()
    fill_screen(mask_ref, screen_ref, me)

    def column_step(p, carry):
        whole(*forth, p).wait_recv()
        column_stage(in_forth.at[p], screen_ref, x_forth_ref, x_back_ref, out_back.at[p])
        in_back[p, me] = out_back[p, me]
        send(*back, p)
        return carry

    lax.fori_loop(0, count, column_step, 0)

    def backward_step(p, carry):
        whole(*back, p).wait_recv()
        backward_stage(in_back.at[p], fxc_ref, y_back_ref, z_back_ref, result_ref.at[p])
        return carry

    lax.fori_loop(0, count, backward_step, 0)

    def drain(p, carry):
        whole(*forth, p).wait_send()
        whole(*back, p).wait_send()
        return carry

    lax.fori_loop(0, count, drain, 0)


def place_kernel(owner_ref, held_ref, out_ref, sem):
    count = out_ref.shape[0]
    copies = [pltpu.make_async_copy(held_ref.at[owner_ref[slot]], out_ref.at[slot], sem.at[slot]) for slot in range(count)]
    for copy in copies:
        copy.start()
    for copy in copies:
        copy.wait()


def per_device(drho_part, fxc, cutoff_mask, owner_table):
    density = drho_part[0]
    if lax.axis_size("pool") > 1:
        density = lax.psum(density, "pool")
    count, _, width, length, _ = density.shape
    slabs = length // width
    rows, lanes = 2 * width, width * length

    forth, back = complex_dft(length, -1.0), complex_dft(length, 1.0)
    by_slab, by_inner = slab_order(length, width), inner_order(length, width)
    tables = (
        halves(forth.T),
        halves(forth[by_inner]),
        halves(forth[:, by_slab]),
        halves(back[by_slab]),
        halves(back[:, by_inner]),
        halves(back.T),
    )
    tables = [jnp.asarray(table) for table in tables]

    packed = pltpu.VMEM((count, slabs, rows, lanes), jnp.float32)
    held = pl.pallas_call(
        exchange_kernel,
        out_shape=pltpu.VMEM(density.shape, jnp.float32),
        in_specs=[pl.BlockSpec(memory_space=pl.ANY)] * 9,
        out_specs=pl.BlockSpec(memory_space=pltpu.VMEM),
        scratch_shapes=[packed] * 4
        + [
            pltpu.VMEM((length, lanes), jnp.float32),
            pltpu.VMEM(fxc.shape, jnp.float32),
            pltpu.VMEM(cutoff_mask.shape, jnp.int32),
        ]
        + [pltpu.VMEM(table.shape, table.dtype) for table in tables]
        + [pltpu.SemaphoreType.DMA((count,)), pltpu.SemaphoreType.DMA((8,))]
        + [pltpu.SemaphoreType.DMA((count,))] * 4,
        compiler_params=pltpu.CompilerParams(
            collective_id=0, has_side_effects=True, vmem_limit_bytes=VMEM_MIB * 2**20
        ),
        cost_estimate=pl.CostEstimate(
            flops=count * 144 * rows * lanes * length * slabs // 2,
            bytes_accessed=density.size * 8,
            transcendentals=0,
        ),
    )(density, fxc, cutoff_mask, *tables)

    return pl.pallas_call(
        place_kernel,
        out_shape=jax.ShapeDtypeStruct(density.shape, jnp.float32),
        in_specs=[pl.BlockSpec(memory_space=pltpu.SMEM), pl.BlockSpec(memory_space=pltpu.VMEM)],
        out_specs=pl.BlockSpec(memory_space=pl.ANY),
        scratch_shapes=[pltpu.SemaphoreType.DMA((count,))],
        compiler_params=pltpu.CompilerParams(vmem_limit_bytes=2**20),
        cost_estimate=pl.CostEstimate(flops=0, bytes_accessed=density.size * 8, transcendentals=0),
    )(owner_table, held)


def solution(mesh):
    placed = (
        P("pool", "group", None, "slab", None, None),
        P("slab", None, None),
        P(None, "slab", None),
        P("group"),
    )
    return jax.shard_map(
        per_device,
        mesh=mesh,
        in_specs=placed,
        out_specs=P("group", None, "slab", None, None),
        check_vma=False,
    )
```

time: 415 us -> 372 us (0.90)
  waiting for transfers between devices: 336 us -> 0 us
  Pallas kernels: 51.7 us -> 370 us
  starting transfers between devices: 22.3 us -> 0 us
    all_to_all x4 -> x0, waiting for transfers between devices: 336 us -> none  [swap(): lax.all_to_all(field, 'slab', split_axis=0, concat_axis=0, tiled=True)]
    pallas_call x6 -> x2, Pallas kernels: 51.7 us -> 370 us  [the longest x1 366 us: per_device(): pl.pallas_call(exchange_kernel, out_shape=pltpu.VMEM(density.shape, jnp.f...]
    all_to_all x4 -> x0, starting transfers between devices: 22.3 us -> none  [swap(): lax.all_to_all(field, 'slab', split_axis=0, concat_axis=0, tiled=True)]
  transfers between devices with their start and end apart: 4 -> 0, of which waited for: 4 -> 0; matrix products, arithmetic and copies ran while one was open for 0% -> 0% of each run, Pallas kernels for 8% -> 0%
where the time goes in v1:
time: 372 us; the launch traced here: 370 us
  Pallas kernels  370 us (99%)
    pallas_call x1, Pallas kernels, per_device(): pl.pallas_call(exchange_kernel, out_shape=pltpu.VMEM(density.shape, jnp.f...  366 us

profile of v1, /device:TPU:24, one launch (start us, length us, event | category | flops | bytes accessed | tf_op | source)
XLA Modules:
  0.0 370.0 jit_solution(7936968039587566583)
XLA Ops:
  0.0 0.0 copy-start
  0.0 366.1 %shard_map.100.held_ref = f32[16,2,4,128,128]{4,3,2,1,0:T(8,128)S(1)} custom-call(f32[16,2,4,128,128]{4,3,2,1,0:T(8,128)} %bitcast.1, f32[4,128,128]{2,1,0:T(8,128)} %fxc_hbm.1, s32[128,4,128]{2,1,0:T(4,128)} %mask_hbm.1, bf16[2,256,256]{2,1,0:T(8,128)(2,1)} %constant.12.clone.z_forth_hbm, bf16[2,256,256]{2,1,0:T(8,128)(2,1)} %constant.13.clone.y_forth_hbm, ...), custom_call_target="tpu_custom_call" | custom-call | flops 19327352832 | bytes 16777216 | tf_op jit(solution)/shard_map/pallas_call | solution.py:315
  366.1 0.0 copy-done
  366.1 4.0 %shard_map.101 = f32[16,2,4,128,128]{4,3,2,1,0:T(8,128)} custom-call(s32[16]{0:T(128)S(1)} %copy-done, f32[16,2,4,128,128]{4,3,2,1,0:T(8,128)S(1)} %shard_map.100.held_ref), custom_call_target="tpu_custom_call" | custom-call | bytes 16777216 | tf_op jit(solution)/shard_map/pallas_call | solution.py:339
Async XLA Ops:
  0.0 366.1 %copy-start = (s32[16]{0:T(128)S(1)}, s32[16]{0:T(128)}, u32[]{:S(2)}) copy-start(s32[16]{0:T(128)} %owner_ref.1) | copy-start | bytes 196

commit v2 on v1

v2 whole, which is shorter than its diff:
```python
import functools
import math

import jax
import jax.numpy as jnp
import numpy as np
from jax import lax
from jax.experimental import pallas as pl
from jax.experimental.pallas import tpu as pltpu
from jax.sharding import PartitionSpec as P

VMEM_MIB = 40
PLACE_MIB = 8
EARLY = 2
MESH = pl.DeviceIdType.MESH


def halves(matrix):
    high = matrix.astype(np.float32).astype(jnp.bfloat16)
    low = (matrix - high.astype(np.float64)).astype(np.float32).astype(jnp.bfloat16)
    return np.stack([high, low])


def complex_dft(length, sign):
    index = np.arange(length)
    angle = (index[:, None] * index[None, :] % length) * (2.0 * math.pi / length)
    cosine, sine = np.cos(angle), sign * np.sin(angle)
    return np.block([[cosine, -sine], [sine, cosine]])


def slab_order(length, width):
    table = np.arange(2 * length).reshape(2, length // width, width)
    return table.transpose(1, 0, 2).reshape(-1)


def inner_order(length, width):
    table = np.arange(2 * length).reshape(2, length // width, width)
    return table.transpose(2, 0, 1).reshape(-1)


def split(value):
    high = value.astype(jnp.bfloat16)
    low = (value - high.astype(jnp.float32)).astype(jnp.bfloat16)
    return high, low


def dot(left, right):
    return jnp.dot(left, right, preferred_element_type=jnp.float32)


def left_dot(matrix_ref, value):
    high, low = split(value)
    return dot(matrix_ref[0], high) + (dot(matrix_ref[1], high) + dot(matrix_ref[0], low))


def right_dot(value, matrix_ref):
    high, low = split(value)
    return dot(high, matrix_ref[0]) + (dot(low, matrix_ref[0]) + dot(high, matrix_ref[1]))


def forward_stage(field_ref, along_y_ref, out_ref):
    _, width, length, _ = field_ref.shape
    slabs = length // width
    field = jnp.concatenate(
        [jnp.concatenate([field_ref[c, x] for x in range(width)], axis=1) for c in range(2)], axis=0
    )
    field = left_dot(along_y_ref, field)
    for y in range(width):
        for c in range(2):
            first = (y * 2 + c) * slabs
            for x in range(width):
                out_ref[:, c * width + x, y * length : (y + 1) * length] = field[
                    first : first + slabs, x * length : (x + 1) * length
                ]


def column_stage(field_ref, screen_ref, x_forth_ref, z_forth_ref, z_back_ref, x_back_ref, out_ref):
    slabs, rows, lanes = field_ref.shape
    length = screen_ref.shape[1]
    width = lanes // length
    field = left_dot(x_forth_ref, field_ref[...].reshape(slabs * rows, lanes))
    field = jnp.concatenate(
        [
            jnp.concatenate(
                [field[c * length : (c + 1) * length, y * length : (y + 1) * length] for c in range(2)], axis=1
            )
            for y in range(width)
        ],
        axis=0,
    )
    field = right_dot(field, z_forth_ref)
    screen = screen_ref[...]
    field = jnp.concatenate([field[:, :length] * screen, field[:, length:] * screen], axis=1)
    field = right_dot(field, z_back_ref)
    field = jnp.concatenate(
        [
            jnp.concatenate(
                [field[y * length : (y + 1) * length, c * length : (c + 1) * length] for y in range(width)], axis=1
            )
            for c in range(2)
        ],
        axis=0,
    )
    out_ref[...] = left_dot(x_back_ref, field).reshape(slabs, rows, lanes)


def backward_stage(field_ref, fxc_ref, along_y_ref, density_ref, out_ref):
    _, width, length, _ = out_ref.shape
    field = jnp.concatenate(
        [
            jnp.concatenate(
                [field_ref[:, c * width + x, y * length : (y + 1) * length] for y in range(width) for c in range(2)],
                axis=0,
            )
            for x in range(width)
        ],
        axis=1,
    )
    field = left_dot(along_y_ref, field)
    for c in range(2):
        for x in range(width):
            part = field[c * length : (c + 1) * length, x * length : (x + 1) * length]
            out_ref[c, x] = part + fxc_ref[x] * density_ref[c, x]


def frequency(index, length):
    return (lax.rem(index + length // 2, length) - length // 2).astype(jnp.float32)


def fill_screen(mask_ref, screen_ref, me):
    length, width, _ = mask_ref.shape
    shape = (length, length)
    unit = (2.0 * math.pi / length) ** 2
    along_x = frequency(lax.broadcasted_iota(jnp.int32, shape, 0), length)
    along_z = frequency(lax.broadcasted_iota(jnp.int32, shape, 1), length)
    plane = along_x * along_x + along_z * along_z
    for y in range(width):
        along_y = frequency(jnp.full(shape, me * width + y, jnp.int32), length)
        total = unit * (plane + along_y * along_y) + 0.25
        kept = mask_ref[:, y, :].astype(jnp.float32)
        screen_ref[y * length : (y + 1) * length, :] = 4.0 * math.pi * kept / total * (1.0 / float(length**3))


def peer_steps(slabs):
    if slabs & (slabs - 1):
        return [], list(range(1, slabs))
    half = slabs // 2
    order = [0, 6, 2, 4, 1, 7, 3, 5]
    order = [base + k for base in range(0, half, 8) for k in order if base + k < half]
    steps = [step for k in order for step in (half + k, k) if step]
    inner = 2 ** -(-(slabs.bit_length() - 1) // 2)
    near = [step for step in steps if step < inner or step % inner < 2]
    near.sort(key=lambda step: step < half)
    return near, steps


def exchange_kernel(
    density_ref,
    fxc_hbm,
    mask_hbm,
    y_forth_hbm,
    x_forth_hbm,
    z_forth_hbm,
    z_back_hbm,
    x_back_hbm,
    y_back_hbm,
    result_ref,
    in_back,
    fxc_ref,
    y_back_ref,
    out_forth,
    in_forth,
    out_back,
    screen_ref,
    mask_ref,
    y_forth_ref,
    x_forth_ref,
    z_forth_ref,
    z_back_ref,
    x_back_ref,
    load_sem,
    table_sem,
    out_forth_sem,
    in_forth_sem,
    out_back_sem,
    in_back_sem,
    ready_sem,
):
    count, slabs, _, _ = out_forth.shape
    me = lax.axis_index("slab")
    near, steps = peer_steps(slabs)
    far = [step for step in steps if step not in near]
    early = min(EARLY, count) if near and far else 0

    def peer_of(step):
        return lax.bitwise_xor(me, step) if near else lax.rem(me + step, slabs)

    def load(p):
        return pltpu.make_async_copy(density_ref.at[p], result_ref.at[p], load_sem.at[p])

    pairs = (
        (y_forth_hbm, y_forth_ref),
        (mask_hbm, mask_ref),
        (x_forth_hbm, x_forth_ref),
        (z_forth_hbm, z_forth_ref),
        (z_back_hbm, z_back_ref),
        (x_back_hbm, x_back_ref),
        (fxc_hbm, fxc_ref),
        (y_back_hbm, y_back_ref),
    )
    tables = [pltpu.make_async_copy(source, target, table_sem.at[k]) for k, (source, target) in enumerate(pairs)]

    def signal(semaphore, chosen):
        for step in chosen:
            pl.semaphore_signal(semaphore, inc=1, device_id={"slab": peer_of(step)}, device_id_type=MESH)

    def send(source, target, out_sem, in_sem, p, chosen):
        for step in chosen:
            peer = peer_of(step)
            pltpu.make_async_remote_copy(
                source.at[p, peer],
                target.at[p, me],
                out_sem.at[p],
                in_sem.at[p],
                device_id={"slab": peer},
                device_id_type=MESH,
            ).start()

    def whole(source, target, out_sem, in_sem, p):
        others = pl.ds(0, slabs - 1)
        return pltpu.make_async_remote_copy(
            source.at[p, others],
            target.at[p, others],
            out_sem.at[p],
            in_sem.at[p],
            device_id={"slab": me},
            device_id_type=MESH,
        )

    forth = (out_forth, in_forth, out_forth_sem, in_forth_sem)
    back = (out_back, in_back, out_back_sem, in_back_sem)

    barrier = pltpu.get_barrier_semaphore()
    greeted = near if early else steps
    load(0).start()
    tables[0].start()
    signal(barrier, greeted)

    def load_rest(p, carry):
        load(p).start()
        return carry

    lax.fori_loop(1, count, load_rest, 0)
    for table in tables[1:]:
        table.start()

    def forward(p):
        load(p).wait()
        forward_stage(result_ref.at[p], y_forth_ref, out_forth.at[p])
        in_forth[p, me] = out_forth[p, me]

    tables[0].wait()

    def early_step(p, carry):
        forward(p)

        @pl.when(p == 0)
        def _():
            pl.semaphore_wait(barrier, len(greeted))
            signal(ready_sem, near)

        send(*forth, p, near)
        return carry

    def early_rest(p, carry):
        send(*forth, p, far)
        return carry

    def forward_step(p, carry):
        forward(p)
        if not early:

            @pl.when(p == 0)
            def _():
                pl.semaphore_wait(barrier, len(greeted))

        send(*forth, p, steps)
        return carry

    if early:
        lax.fori_loop(0, early, early_step, 0)
        pl.semaphore_wait(ready_sem, len(near))
        lax.fori_loop(0, early, early_rest, 0)
    lax.fori_loop(early, count, forward_step, 0)

    for table in tables[1:]:
        table.wait()
    fill_screen(mask_ref, screen_ref, me)

    def column_step(p, carry):
        whole(*forth, p).wait_recv()
        column_stage(in_forth.at[p], screen_ref, x_forth_ref, z_forth_ref, z_back_ref, x_back_ref, out_back.at[p])
        in_back[p, me] = out_back[p, me]
        send(*back, p, steps)
        return carry

    lax.fori_loop(0, count, column_step, 0)

    def backward_step(p, carry):
        whole(*back, p).wait_recv()
        backward_stage(in_back.at[p], fxc_ref, y_back_ref, result_ref.at[p], result_ref.at[p])
        return carry

    lax.fori_loop(0, count - 1, backward_step, 0)

    def drain(p, carry):
        whole(*forth, p).wait_send()
        whole(*back, p).wait_send()
        return carry

    lax.fori_loop(0, count, drain, 0)
    whole(*back, count - 1).wait_recv()


def place_kernel(owner_ref, held_ref, in_back, fxc_ref, y_back_ref, out_ref, final_ref, sem):
    count = out_ref.shape[0]
    last = count - 1
    owner = [owner_ref[0, slot] for slot in range(count)]
    for slot in range(count):
        copy = pltpu.make_async_copy(held_ref.at[owner[slot]], out_ref.at[slot], sem.at[slot])
        pl.when(owner[slot] != last)(copy.start)
    backward_stage(in_back.at[last], fxc_ref, y_back_ref, held_ref.at[last], final_ref)
    for slot in range(count):
        copy = pltpu.make_async_copy(final_ref, out_ref.at[slot], sem.at[slot])
        pl.when(owner[slot] == last)(copy.start)
    for slot in range(count):
        pltpu.make_async_copy(final_ref, out_ref.at[slot], sem.at[slot]).wait()


def per_device(drho_part, fxc, cutoff_mask, owner_table):
    density = drho_part[0]
    if lax.axis_size("pool") > 1:
        density = lax.psum(density, "pool")
    count, _, width, length, _ = density.shape
    slabs = length // width
    rows, lanes = 2 * width, width * length

    forth, back = complex_dft(length, -1.0), complex_dft(length, 1.0)
    by_slab, by_inner = slab_order(length, width), inner_order(length, width)
    tables = (
        halves(forth[by_inner]),
        halves(forth[:, by_slab]),
        halves(forth.T),
        halves(back.T),
        halves(back[by_slab]),
        halves(back[:, by_inner]),
    )
    tables = [jnp.asarray(table) for table in tables]

    packed = pltpu.VMEM((count, slabs, rows, lanes), jnp.float32)
    placed = [pltpu.VMEM(table.shape, table.dtype) for table in tables]
    whole_fxc = pltpu.VMEM(fxc.shape, jnp.float32)
    in_vmem = pl.BlockSpec(memory_space=pltpu.VMEM)
    anywhere = pl.BlockSpec(memory_space=pl.ANY)
    work = 48 * rows * lanes * length * slabs // 2
    kept = pl.pallas_call(
        exchange_kernel,
        out_shape=[pltpu.VMEM(density.shape, jnp.float32), packed, whole_fxc, placed[5]],
        in_specs=[anywhere] * 9,
        out_specs=[in_vmem] * 4,
        scratch_shapes=[packed] * 3
        + [pltpu.VMEM((lanes, length), jnp.float32), pltpu.VMEM(cutoff_mask.shape, jnp.int32)]
        + placed[:5]
        + [pltpu.SemaphoreType.DMA((count,)), pltpu.SemaphoreType.DMA((8,))]
        + [pltpu.SemaphoreType.DMA((count,))] * 4
        + [pltpu.SemaphoreType.REGULAR],
        compiler_params=pltpu.CompilerParams(
            collective_id=0, has_side_effects=True, vmem_limit_bytes=VMEM_MIB * 2**20
        ),
        cost_estimate=pl.CostEstimate(flops=3 * count * work, bytes_accessed=density.size * 4, transcendentals=0),
    )(density, fxc, cutoff_mask, *tables)

    return pl.pallas_call(
        place_kernel,
        out_shape=jax.ShapeDtypeStruct(density.shape, jnp.float32),
        in_specs=[in_vmem] * 5,
        out_specs=anywhere,
        scratch_shapes=[pltpu.VMEM(density.shape[1:], jnp.float32), pltpu.SemaphoreType.DMA((count,))],
        compiler_params=pltpu.CompilerParams(vmem_limit_bytes=PLACE_MIB * 2**20),
        cost_estimate=pl.CostEstimate(flops=work, bytes_accessed=density.size * 4, transcendentals=0),
    )(owner_table.reshape(1, count), *kept)


def solution(mesh):
    placed = (
        P("pool", "group", None, "slab", None, None),
        P("slab", None, None),
        P(None, "slab", None),
        P("group"),
    )
    return jax.shard_map(
        per_device,
        mesh=mesh,
        in_specs=placed,
        out_specs=P("group", None, "slab", None, None),
        check_vma=False,
    )
```

time: 372 us -> 370 us (level)
  Pallas kernels: 370 us -> 366 us
where the time goes in v2:
time: 370 us; the launch traced here: 366 us
  Pallas kernels  366 us (99%)
    pallas_call x1, Pallas kernels, per_device(): pl.pallas_call(exchange_kernel, out_shape=[pltpu.VMEM(density.shape, jnp....  363 us

profile of v2, /device:TPU:24, one launch (start us, length us, event | category | flops | bytes accessed | tf_op | source)
XLA Modules:
  0.0 366.5 jit_solution(6638451283482170711)
XLA Ops:
  0.0 0.0 copy-start
  0.0 362.7 %shard_map.100 = (f32[16,2,4,128,128]{4,3,2,1,0:T(8,128)S(1)}, f32[16,32,8,512]{3,2,1,0:T(8,128)S(1)}, f32[4,128,128]{2,1,0:T(8,128)S(1)}, bf16[2,256,256]{2,1,0:T(8,128)(2,1)S(1)}) custom-call(f32[16,2,4,128,128]{4,3,2,1,0:T(8,128)} %bitcast.3, f32[4,128,128]{2,1,0:T(8,128)} %fxc_hbm.1, s32[128,4,128]{2,1,0:T(4,128)} %mask_hbm.1, ...), custom_call_target="tpu_custom_call" | custom-call | flops 19327352832 | bytes 8388608 | tf_op jit(solution)/shard_map/pallas_call | solution.py:366
  362.7 0.0 copy-done
  362.7 3.8 %shard_map.101 = f32[16,2,4,128,128]{4,3,2,1,0:T(8,128)} custom-call(s32[1,16]{1,0:T(1,128)S(1)} %bitcast.2, f32[16,2,4,128,128]{4,3,2,1,0:T(8,128)S(1)} %get-tuple-element.9.held_ref, f32[16,32,8,512]{3,2,1,0:T(8,128)S(1)} %get-tuple-element.10.in_back, f32[4,128,128]{2,1,0:T(8,128)S(1)} %get-tuple-element.11.fxc_ref, ...), custom_call_target="tpu_custom_call" | custom-call | flops 402653184 | bytes 8388608 | tf_op jit(solution)/shard_map/pallas_call | solution.py:383
Async XLA Ops:
  0.0 362.7 %copy-start = (s32[16]{0:T(128)S(1)}, s32[16]{0:T(128)}, u32[]{:S(2)}) copy-start(s32[16]{0:T(128)} %param.13) | copy-start | bytes 196

commit v3 on v2

--- a/solution.py
+++ b/solution.py
@@ -145,7 +145,7 @@
     if slabs & (slabs - 1):
         return [], list(range(1, slabs))
     half = slabs // 2
-    order = [0, 6, 2, 4, 1, 7, 3, 5]
+    order = [0, 7, 2, 5, 6, 1, 4, 3]
     order = [base + k for base in range(0, half, 8) for k in order if base + k < half]
     steps = [step for k in order for step in (half + k, k) if step]
     inner = 2 ** -(-(slabs.bit_length() - 1) // 2)
@@ -192,8 +192,14 @@
     far = [step for step in steps if step not in near]
     early = min(EARLY, count) if near and far else 0
 
+    half, quarter = slabs // 2, slabs // 4
+
     def peer_of(step):
-        return lax.bitwise_xor(me, step) if near else lax.rem(me + step, slabs)
+        if not near:
+            return lax.rem(me + step, slabs)
+        if step < half:
+            return lax.bitwise_xor(me, step)
+        return lax.bitwise_xor(lax.bitwise_xor(me, step), lax.bitwise_and(me, quarter))
 
     def load(p):
         return pltpu.make_async_copy(density_ref.at[p], result_ref.at[p], load_sem.at[p])
@@ -242,8 +248,9 @@
 
     barrier = pltpu.get_barrier_semaphore()
     greeted = near if early else steps
-    load(0).start()
-    tables[0].start()
+    for c in range(2):
+        pltpu.make_async_copy(density_ref.at[0, c], result_ref.at[0, c], load_sem.at[0]).start()
+        pltpu.make_async_copy(y_forth_hbm.at[c], y_forth_ref.at[c], table_sem.at[0]).start()
     signal(barrier, greeted)
 
     def load_rest(p, carry):

time: 370 us -> 370 us (level)
  Pallas kernels: 366 us -> 370 us
where the time goes in v3:
time: 370 us
  Pallas kernels  370 us (100%)
    pallas_call x1, Pallas kernels, per_device(): pl.pallas_call(exchange_kernel, out_shape=[pltpu.VMEM(density.shape, jnp....  366 us

profile of v3, /device:TPU:24, one launch (start us, length us, event | category | flops | bytes accessed | tf_op | source)
XLA Modules:
  0.0 370.0 jit_solution(11490818304092902265)
XLA Ops:
  0.0 0.0 copy-start
  0.0 366.2 %shard_map.100 = (f32[16,2,4,128,128]{4,3,2,1,0:T(8,128)S(1)}, f32[16,32,8,512]{3,2,1,0:T(8,128)S(1)}, f32[4,128,128]{2,1,0:T(8,128)S(1)}, bf16[2,256,256]{2,1,0:T(8,128)(2,1)S(1)}) custom-call(f32[16,2,4,128,128]{4,3,2,1,0:T(8,128)} %bitcast.3, f32[4,128,128]{2,1,0:T(8,128)} %fxc_hbm.1, s32[128,4,128]{2,1,0:T(4,128)} %mask_hbm.1, ...), custom_call_target="tpu_custom_call" | custom-call | flops 19327352832 | bytes 8388608 | tf_op jit(solution)/shard_map/pallas_call | solution.py:373
  366.2 0.0 copy-done
  366.2 3.8 %shard_map.101 = f32[16,2,4,128,128]{4,3,2,1,0:T(8,128)} custom-call(s32[1,16]{1,0:T(1,128)S(1)} %bitcast.2, f32[16,2,4,128,128]{4,3,2,1,0:T(8,128)S(1)} %get-tuple-element.9.held_ref, f32[16,32,8,512]{3,2,1,0:T(8,128)S(1)} %get-tuple-element.10.in_back, f32[4,128,128]{2,1,0:T(8,128)S(1)} %get-tuple-element.11.fxc_ref, ...), custom_call_target="tpu_custom_call" | custom-call | flops 402653184 | bytes 8388608 | tf_op jit(solution)/shard_map/pallas_call | solution.py:390
Async XLA Ops:
  0.0 366.2 %copy-start = (s32[16]{0:T(128)S(1)}, s32[16]{0:T(128)}, u32[]{:S(2)}) copy-start(s32[16]{0:T(128)} %param.13) | copy-start | bytes 196

commit v4 on v3

--- a/solution.py
+++ b/solution.py
@@ -58,16 +58,17 @@
     return dot(high, matrix_ref[0]) + (dot(low, matrix_ref[0]) + dot(high, matrix_ref[1]))
 
 
-def forward_stage(field_ref, along_y_ref, out_ref):
+def forward_stage(field_ref, along_y_ref, out_ref, begin=0, end=None):
     _, width, length, _ = field_ref.shape
     slabs = length // width
+    end = width if end is None else end
     field = jnp.concatenate(
         [jnp.concatenate([field_ref[c, x] for x in range(width)], axis=1) for c in range(2)], axis=0
     )
-    field = left_dot(along_y_ref, field)
-    for y in range(width):
+    field = left_dot(along_y_ref.at[:, 2 * slabs * begin : 2 * slabs * end], field)
+    for y in range(begin, end):
         for c in range(2):
-            first = (y * 2 + c) * slabs
+            first = ((y - begin) * 2 + c) * slabs
             for x in range(width):
                 out_ref[:, c * width + x, y * length : (y + 1) * length] = field[
                     first : first + slabs, x * length : (x + 1) * length
@@ -220,12 +221,12 @@
         for step in chosen:
             pl.semaphore_signal(semaphore, inc=1, device_id={"slab": peer_of(step)}, device_id_type=MESH)
 
-    def send(source, target, out_sem, in_sem, p, chosen):
+    def send(source, target, out_sem, in_sem, p, chosen, part=slice(None)):
         for step in chosen:
             peer = peer_of(step)
             pltpu.make_async_remote_copy(
-                source.at[p, peer],
-                target.at[p, me],
+                source.at[p, peer, :, part],
+                target.at[p, me, :, part],
                 out_sem.at[p],
                 in_sem.at[p],
                 device_id={"slab": peer},
@@ -270,12 +271,6 @@
 
     def early_step(p, carry):
         forward(p)
-
-        @pl.when(p == 0)
-        def _():
-            pl.semaphore_wait(barrier, len(greeted))
-            signal(ready_sem, near)
-
         send(*forth, p, near)
         return carry
 
@@ -295,7 +290,18 @@
         return carry
 
     if early:
-        lax.fori_loop(0, early, early_step, 0)
+        width, length, lanes = density_ref.shape[2], density_ref.shape[3], out_forth.shape[3]
+        middle = max(width // 2, 1)
+        load(0).wait()
+        for begin, end in ((0, middle), (middle, width)):
+            if begin < end:
+                forward_stage(result_ref.at[0], y_forth_ref, out_forth.at[0], begin, end)
+                if begin == 0:
+                    pl.semaphore_wait(barrier, len(greeted))
+                    signal(ready_sem, near)
+                send(*forth, 0, near, slice(begin * length, end * length))
+        in_forth[0, me] = out_forth[0, me]
+        lax.fori_loop(1, early, early_step, 0)
         pl.semaphore_wait(ready_sem, len(near))
         lax.fori_loop(0, early, early_rest, 0)
     lax.fori_loop(early, count, forward_step, 0)

time: 370 us -> 370 us (level)
  no operation moved by 1% of the time
where the time goes in v4:
time: 370 us
  Pallas kernels  370 us (100%)
    pallas_call x1, Pallas kernels, per_device(): pl.pallas_call(exchange_kernel, out_shape=[pltpu.VMEM(density.shape, jnp....  366 us

profile of v4, /device:TPU:24, one launch (start us, length us, event | category | flops | bytes accessed | tf_op | source)
XLA Modules:
  0.0 370.1 jit_solution(12718844846225037287)
XLA Ops:
  0.0 0.0 copy-start
  0.0 366.2 %shard_map.100 = (f32[16,2,4,128,128]{4,3,2,1,0:T(8,128)S(1)}, f32[16,32,8,512]{3,2,1,0:T(8,128)S(1)}, f32[4,128,128]{2,1,0:T(8,128)S(1)}, bf16[2,256,256]{2,1,0:T(8,128)(2,1)S(1)}) custom-call(f32[16,2,4,128,128]{4,3,2,1,0:T(8,128)} %bitcast.3, f32[4,128,128]{2,1,0:T(8,128)} %fxc_hbm.1, s32[128,4,128]{2,1,0:T(4,128)} %mask_hbm.1, ...), custom_call_target="tpu_custom_call" | custom-call | flops 19327352832 | bytes 8388608 | tf_op jit(solution)/shard_map/pallas_call | solution.py:379
  366.3 0.0 copy-done
  366.3 3.8 %shard_map.101 = f32[16,2,4,128,128]{4,3,2,1,0:T(8,128)} custom-call(s32[1,16]{1,0:T(1,128)S(1)} %bitcast.2, f32[16,2,4,128,128]{4,3,2,1,0:T(8,128)S(1)} %get-tuple-element.9.held_ref, f32[16,32,8,512]{3,2,1,0:T(8,128)S(1)} %get-tuple-element.10.in_back, f32[4,128,128]{2,1,0:T(8,128)S(1)} %get-tuple-element.11.fxc_ref, ...), custom_call_target="tpu_custom_call" | custom-call | flops 402653184 | bytes 8388608 | tf_op jit(solution)/shard_map/pallas_call | solution.py:396
Async XLA Ops:
  0.0 366.3 %copy-start = (s32[16]{0:T(128)S(1)}, s32[16]{0:T(128)}, u32[]{:S(2)}) copy-start(s32[16]{0:T(128)} %param.13) | copy-start | bytes 196

commit v5 on v4

--- a/solution.py
+++ b/solution.py
@@ -258,15 +258,19 @@
         load(p).start()
         return carry
 
-    lax.fori_loop(1, count, load_rest, 0)
-    for table in tables[1:]:
-        table.start()
+    soon = max(min(early, count), 1)
+    lax.fori_loop(1, soon, load_rest, 0)
 
     def forward(p):
         load(p).wait()
         forward_stage(result_ref.at[p], y_forth_ref, out_forth.at[p])
         in_forth[p, me] = out_forth[p, me]
 
+    def load_later():
+        lax.fori_loop(soon, count, load_rest, 0)
+        for table in tables[1:]:
+            table.start()
+
     tables[0].wait()
 
     def early_step(p, carry):
@@ -293,6 +297,7 @@
         width, length, lanes = density_ref.shape[2], density_ref.shape[3], out_forth.shape[3]
         middle = max(width // 2, 1)
         load(0).wait()
+        load_later()
         for begin, end in ((0, middle), (middle, width)):
             if begin < end:
                 forward_stage(result_ref.at[0], y_forth_ref, out_forth.at[0], begin, end)
@@ -304,6 +309,8 @@
         lax.fori_loop(1, early, early_step, 0)
         pl.semaphore_wait(ready_sem, len(near))
         lax.fori_loop(0, early, early_rest, 0)
+    else:
+        load_later()
     lax.fori_loop(early, count, forward_step, 0)
 
     for table in tables[1:]:

time: 370 us -> 370 us (level)
  no operation moved by 1% of the time
where the time goes in v5:
time: 370 us
  Pallas kernels  370 us (100%)
    pallas_call x1, Pallas kernels, per_device(): pl.pallas_call(exchange_kernel, out_shape=[pltpu.VMEM(density.shape, jnp....  366 us

profile of v5, /device:TPU:24, one launch (start us, length us, event | category | flops | bytes accessed | tf_op | source)
XLA Modules:
  0.0 370.0 jit_solution(9743934279391113210)
XLA Ops:
  0.0 0.0 copy-start
  0.0 366.2 %shard_map.100 = (f32[16,2,4,128,128]{4,3,2,1,0:T(8,128)S(1)}, f32[16,32,8,512]{3,2,1,0:T(8,128)S(1)}, f32[4,128,128]{2,1,0:T(8,128)S(1)}, bf16[2,256,256]{2,1,0:T(8,128)(2,1)S(1)}) custom-call(f32[16,2,4,128,128]{4,3,2,1,0:T(8,128)} %bitcast.3, f32[4,128,128]{2,1,0:T(8,128)} %fxc_hbm.1, s32[128,4,128]{2,1,0:T(4,128)} %mask_hbm.1, ...), custom_call_target="tpu_custom_call" | custom-call | flops 19327352832 | bytes 8388608 | tf_op jit(solution)/shard_map/pallas_call | solution.py:386
  366.2 0.0 copy-done
  366.3 3.8 %shard_map.101 = f32[16,2,4,128,128]{4,3,2,1,0:T(8,128)} custom-call(s32[1,16]{1,0:T(1,128)S(1)} %bitcast.2, f32[16,2,4,128,128]{4,3,2,1,0:T(8,128)S(1)} %get-tuple-element.9.held_ref, f32[16,32,8,512]{3,2,1,0:T(8,128)S(1)} %get-tuple-element.10.in_back, f32[4,128,128]{2,1,0:T(8,128)S(1)} %get-tuple-element.11.fxc_ref, ...), custom_call_target="tpu_custom_call" | custom-call | flops 402653184 | bytes 8388608 | tf_op jit(solution)/shard_map/pallas_call | solution.py:403
Async XLA Ops:
  0.0 366.3 %copy-start = (s32[16]{0:T(128)S(1)}, s32[16]{0:T(128)}, u32[]{:S(2)}) copy-start(s32[16]{0:T(128)} %param.13) | copy-start | bytes 196
